TPU v7x, 32 devices: a whole 2x2x4 slice. The times are simulated.
32 devices in a mesh: date: 16 (over z, y, x), prod: 2 (over core).
Axes of the slice: x: 2, y: 2, z: 4, core: 2. Of those that a mesh axis runs over, the one named last changes fastest.
Arguments:
- daily_sales: float32 [256, 512, 128], P('prod', 'date'), may hold values from -2.5 to 2.5
- week_id: int32 [512], P('date'), may hold values from 0 to 102, never falling along the last dimension, each value on 1 to 7 neighbouring positions
- month_id: int32 [512], P('date'), may hold values from 0 to 21, never falling along the last dimension, each value on 1 to 31 neighbouring positions
- year_id: int32 [512], P('date'), may hold values from 0 to 1, never falling along the last dimension, each value on 1 to 366 neighbouring positions
Outputs:
- running: float32 [256, 512, 128], P('prod', 'date')
- week_total: float32 [256, 512, 128], P('prod', 'date')
- month_total: float32 [256, 512, 128], P('prod', 'date')
- year_total: float32 [256, 512, 128], P('prod', 'date')
- store_rollup: float32 [4, 512, 128], P(None, 'date')
Inputs may be any that keep to these rules, and one draw needn't show every extreme that they name: `week_id`: starts at 0 and never falls along the dates; each week covers 1 to 7 consecutive dates and some cover exactly 7. `month_id`: starts at 0 and never falls along the dates; each month covers 1 to 31 consecutive dates and some cover exactly 31; months need not line up with weeks. `year_id`: starts at 0 and never falls along the dates; each year covers 1 to 366 consecutive dates and some cover exactly 366; years need not line up with weeks or months.
All inputs are finite; a program needn't handle non-finite values.
Results may differ from a plain program's by a relative error of at most 0.000094.
Values sent between devices are 32-bit elements.
A program may use at most 64 MiB of HBM per device.

v0:
```python
import jax
import jax.numpy as jnp
from jax import lax
from jax.sharding import PartitionSpec as P

far_index = 1 << 30


def from_behind(block, axis, distance):
    devices = range(lax.axis_size(axis))
    route = [(i - distance, i) for i in devices if i - distance in devices]
    return lax.ppermute(block, axis, route)


def carried_in(value, axis, join, neutral, backward):
    count, mine = (lax.axis_size(axis), lax.axis_index(axis))
    pieces = jax.tree.map(lambda part: lax.all_gather(part, axis), value)
    if backward:
        pieces = jax.tree.map(lambda part: part[::-1], pieces)
        mine = count - 1 - mine
    running = jax.tree.map(
        lambda part, zero: jnp.full_like(part, 0) + jnp.asarray(zero, part.dtype), value, neutral
    )

    def step(position, running):
        longer = join(running, jax.tree.map(lambda part: part[position], pieces))
        return jax.tree.map(lambda new, old: jnp.where(position < mine, new, old), longer, running)

    return lax.fori_loop(0, count - 1, step, running)


def forward(earlier, latter):
    top_early, sums_early = earlier
    top_later, sums_later = latter
    inside = (top_later <= top_early)[:, None, None]
    return (jnp.maximum(top_early, top_later), sums_later + jnp.where(inside, sums_early, 0.0))


def backward(earlier, latter):
    low_early, sums_early = earlier
    low_later, sums_later = latter
    inside = (low_later >= low_early)[:, None, None]
    return (jnp.minimum(low_early, low_later), sums_later + jnp.where(inside, sums_early, 0.0))


def match_keep(ids_seen, ids_own, partial_value):
    return jnp.where((ids_seen == ids_own)[:, None, None], partial_value, 0.0)


def local(daily_sales, week_id, month_id, year_id):
    columns = daily_sales.shape[0]
    span_len = daily_sales.shape[1]
    level_ids = jnp.stack([jnp.zeros_like(week_id), week_id, month_id, year_id])
    offsets = lax.iota(jnp.int32, span_len)
    lower = (offsets[None, :] <= offsets[:, None]).astype(jnp.float32)
    matches = (level_ids[1:, :, None] == level_ids[1:, None, :]).astype(jnp.float32)
    mixers = jnp.concatenate([lower[None], matches], axis=0)
    within = jnp.einsum("kij,pjs->kpis", mixers, daily_sales, precision=lax.Precision.HIGHEST)
    tail_sums = within[:, :, -1, :]
    head_sums = within[1:, :, 0, :]
    first_ids = level_ids[:, 0]
    last_ids = level_ids[:, -1]
    left_ids, left_sums = from_behind((last_ids[1:3], tail_sums[1:3]), "date", 1)
    right_ids, right_sums = from_behind((first_ids[1:3], head_sums[0:2]), "date", -1)
    outer_ids = jnp.stack([last_ids[0], last_ids[3]])
    outer_sums = jnp.stack([tail_sums[0], tail_sums[3]])
    start = (jnp.full((2,), -1, jnp.int32), jnp.zeros_like(outer_sums))
    top_prev, sums_prev = carried_in((outer_ids, outer_sums), "date", forward, start, False)
    outer_in = match_keep(top_prev, jnp.stack([first_ids[0], first_ids[3]]), sums_prev)
    finish = (jnp.full((1,), far_index, jnp.int32), jnp.zeros_like(head_sums[2:]))
    low_next, sums_next = carried_in((first_ids[3:], head_sums[2:]), "date", backward, finish, True)
    middle_in = match_keep(left_ids, first_ids[1:3], left_sums)
    carry_in = jnp.concatenate([outer_in[:1], middle_in, outer_in[1:]], axis=0)
    middle_back = match_keep(right_ids, last_ids[1:3], right_sums)
    carry_back = jnp.concatenate(
        [middle_back, match_keep(low_next, last_ids[3:], sums_next)], axis=0
    )
    start_gain = (level_ids[1:] == first_ids[1:, None]).astype(jnp.float32)
    end_gain = (level_ids[1:] == last_ids[1:, None]).astype(jnp.float32)
    running = within[0] + carry_in[0][:, None, :]
    levels = (
        within[1:]
        + carry_in[1:, :, None, :] * start_gain[:, None, :, None]
        + carry_back[:, :, None, :] * end_gain[:, None, :, None]
    )
    product_terms = jnp.concatenate(
        [jnp.sum(running, axis=0)[None], jnp.sum(levels, axis=1)], axis=0
    )
    store_rollup = lax.psum(product_terms, "prod")
    return (running, levels[0, :columns], levels[1, :columns], levels[2, :columns], store_rollup)


def solution(mesh):
    return jax.shard_map(
        local,
        mesh=mesh,
        in_specs=(P("prod", "date", None), P("date"), P("date"), P("date")),
        out_specs=(
            P("prod", "date", None),
            P("prod", "date", None),
            P("prod", "date", None),
            P("prod", "date", None),
            P(None, "date", None),
        ),
        check_vma=False,
    )
```

profile of v0, /device:TPU:0, one launch (start us, length us, event | category | flops | bytes accessed | tf_op | source)
XLA Modules:
  0.0 187.9 jit_solution(4630445050261132228)
XLA Ops:
  7.3 0.8 pad_add_fusion
  8.2 0.7 copy-done
  8.9 3.4 %convolution_bitcast_fusion = f32[4,128,32,128]{3,2,1,0:T(8,128)S(1)} fusion(f32[128,32,128]{2,1,0:T(8,128)S(1)} %copy-done, pred[3,32,32]{2,1,0:T(32,128)(4,1)S(1)} %broadcast_compare_fusion, pred[1,32,32]{2,1,0:T(32,128)(4,1)S(1)} %iota_compare_fusion), kind=kOutput, calls=%fused_computation.11 | convolution fusion | flops 805310464 | bytes 10489856 | tf_op jit(solution)/shard_map/kij,pjs->kpis/dot_general | solution.py:58
  12.3 3.2 %copy-done.1 = f32[4,128,32,128]{3,2,1,0:T(8,128)} copy-done((f32[4,128,32,128]{3,2,1,0:T(8,128)}, f32[4,128,32,128]{3,2,1,0:T(8,128)S(1)}, u32[]{:S(2)}) %copy-start.1) | copy-done | bytes 8388632
  15.5 0.8 fusion.13
  16.6 4.9 %collective-permute-start = (s32[2]{0:T(128)S(1)}, s32[2]{0:T(128)S(1)}, u32[]{:S(2)}, u32[]{:S(2)}) collective-permute-start(s32[2]{0:T(128)S(1)} %get-tuple-element.291), channel_id=1, source_target_pairs={{0,2},{2,4},{4,6},{6,8},{8,10},{10,12},{12,14},{14,16},{16,18},{18... | collective-permute-start | bytes 32 | tf_op jit(solution)/shard_map/ppermute | solution.py:12
  21.5 1.7 fusion.12
  23.2 3.4 %collective-permute-start.1 = (f32[2,128,128]{2,1,0:T(8,128)S(1)}, f32[2,128,128]{2,1,0:T(8,128)S(1)}, u32[]{:S(2)}, u32[]{:S(2)}) collective-permute-start(f32[2,128,128]{2,1,0:T(8,128)S(1)} %bitcast.81), channel_id=1, source_target_pairs={{0,2},{2,4},{4,6},{6,8},{8,10},{10,12},{12,14},{14,16},{16,18},{18... | collective-permute-start | bytes 393224 | tf_op jit(solution)/shard_map/ppermute | solution.py:12
  26.6 1.3 collective-permute-start.2
  27.9 1.3 collective-permute-start.3
  29.2 0.7 pad_maximum_fusion.2
  30.0 0.6 fusion.15
  32.0 0.7 pad_dynamic-update-slice_fusion
  32.8 1.4 bitcast_dynamic-update-slice_fusion
  34.1 17.9 %all-reduce.3 = (s32[32]{0:T(128)S(1)}, s32[16]{0:T(128)S(1)}) all-reduce(s32[32]{0:T(128)S(1)} %pad_dynamic-update-slice_fusion, s32[16]{0:T(128)S(1)} %bitcast_dynamic-update-slice_fusion), channel_id=2, replica_groups=mesh['date'=16,'prod'=2] {'date'}, use_global_device_ids=true, to_apply=%add.1 | all-reduce | flops 48 | bytes 384
  52.5 0.7 broadcast_select_fusion.4
  53.2 21.4 %all-gather.8.cloned.1.call-done = f32[16,128,1,128]{3,1,2,0:T(8,128)} async-done(((f32[1,128,1,128]{3,1,2,0:T(8,128)}), f32[16,128,1,128]{3,1,2,0:T(8,128)}) %all-gather.8.cloned.1.call-update) | async-done | bytes 1048592 | tf_op jit(solution)/shard_map/all_gather | solution.py:17
  74.6 1.3 reverse_bitcast_fusion
  75.9 28.3 %while.33 = (s32[]{:T(128)}, s32[1]{0:T(128)}, f32[1,128,128]{2,1,0:T(8,128)S(1)}, s32[]{:T(128)}, s32[16,1]{0,1:T(1,128)S(1)}, /*index=5*/f32[16,1,128,128]{3,2,1,0:T(8,128)S(1)}, s32[]{:T(128)}, s32[]{:T(128)}) while((s32[]{:T(128)}, s32[1]{0:T(128)}, f32[1,128,128]{2,1,0:T(8,128)S(1)}, s32[]{:T(128)}, s32[16,1]{0,1:T(1,128)S(1)}, ...), condition=%wide.region_3.4_spmd.clone, body=%wide.region_2.3_spmd.clone.sunk | while | flops 65543 | bytes 196764 | solution.py:29
  77.8 0.6 constant_dynamic-slice_fusion.3
  79.7 0.6 constant_dynamic-slice_fusion.3
  83.5 0.6 constant_dynamic-slice_fusion.3
  85.4 0.6 constant_dynamic-slice_fusion.3
  104.8 0.9 pad_maximum_fusion.1
  105.7 31.5 %all-gather.6.cloned.1.call-done = f32[32,128,128]{2,1,0:T(8,128)} async-done(((f32[2,128,128]{2,1,0:T(8,128)}), f32[32,128,128]{2,1,0:T(8,128)}) %all-gather.6.cloned.1.call-update) | async-done | bytes 2097168 | tf_op jit(solution)/shard_map/all_gather | solution.py:17
  137.3 15.9 %while.32 = (s32[]{:T(128)}, s32[2]{0:T(128)S(1)}, f32[2,128,128]{2,1,0:T(8,128)S(1)}, s32[]{:T(128)}, s32[16,2]{1,0:T(8,128)S(1)}, /*index=5*/f32[16,2,128,128]{3,2,1,0:T(8,128)}, s32[]{:T(128)}, s32[]{:T(128)}) while((s32[]{:T(128)}, s32[2]{0:T(128)S(1)}, f32[2,128,128]{2,1,0:T(8,128)S(1)}, s32[]{:T(128)}, ...), condition=%wide.region_1.2_spmd.clone, body=%wide.region_0.1_spmd.clone.sunk | while | flops 131086 | bytes 393380 | solution.py:29
  137.3 1.0 fusion.18
  138.4 1.0 fusion.18
  139.4 1.0 fusion.18
  140.5 1.0 fusion.18
  141.5 1.0 fusion.18
  142.6 1.0 fusion.18
  143.7 1.0 fusion.18
  144.7 1.0 fusion.18
  145.8 1.0 fusion.18
  146.8 1.0 fusion.18
  147.9 1.0 fusion.18
  149.0 1.0 fusion.18
  150.0 1.0 fusion.18
  151.1 1.0 fusion.18
  152.2 1.0 fusion.18
  153.2 0.8 add_compare_fusion
  154.1 3.2 %fusion.8 = (f32[32,128]{1,0:T(8,128)S(1)}, f32[128,32,128]{2,1,0:T(8,128)}) fusion(f32[128,128]{1,0:T(8,128)S(1)} %get-tuple-element.332, f32[4,128,32,128]{3,2,1,0:T(8,128)} %copy-done.1), kind=kLoop, calls=%fused_computation.45 | loop fusion | flops 1044480 | bytes 4276224 | tf_op jit(solution)/shard_map/reduce_sum | solution.py:87
  157.3 5.3 %fusion.10 = (f32[3,32,128]{2,1,0:T(8,128)S(1)}, f32[3,128,32,128]{3,2,1,0:T(8,128)}) fusion(f32[3,32]{1,0:T(4,128)S(1)} %get-tuple-element.334, f32[3,128,128]{2,1,0:T(8,128)S(1)} %pad_maximum_fusion.1, f32[3,32]{1,0:T(4,128)S(1)} %get-tuple-element.333, f32[3,128,128]{2,1,0:T(8,128)S(1)} %pad_maximum_fusion, f32[4,128,32,128]{3,2,1,0:T(8,128)} %copy-done.1), kind=kLoop, calls=%fused_computation.46 | loop fusion | flops 7852032 | bytes 13026048 | tf_op jit(solution)/shard_map/reduce_sum | solution.py:87
  162.5 0.6 pad_maximum_fusion.3
  163.2 5.7 %slice_bitcast_fusion = (f32[128,32,128]{2,1,0:T(8,128)}, f32[128,32,128]{2,1,0:T(8,128)}, f32[128,32,128]{2,1,0:T(8,128)}) fusion(f32[3,128,32,128]{3,2,1,0:T(8,128)} %get-tuple-element.322), kind=kLoop, calls=%fused_computation.12 | loop fusion | bytes 12582912 | tf_op jit(solution)/shard_map/squeeze | solution.py:90
  168.9 10.9 %all-reduce.6.cloned.1.call-done = f32[4,32,128]{2,1,0:T(8,128)} async-done(((f32[4,32,128]{2,1,0:T(8,128)}), f32[4,32,128]{2,1,0:T(8,128)}) %all-reduce.6.cloned.1.call-update) | async-done | bytes 65552 | tf_op jit(solution)/shard_map/psum | solution.py:89
  179.9 1.5 copy.49
  (97 shorter events, 9.0 us)
Async XLA Ops:
  7.2 1.7 copy-start
  7.2 23.6 %copy-start.5 = (u32[32]{0:T(128)S(1)}, u32[32]{0:T(128)}, u32[]{:S(2)}) copy-start(u32[32]{0:T(128)} %constant.81) | copy-start | bytes 388
  7.2 9.2 %copy-start.4 = (s32[32]{0:T(128)S(1)}, s32[32]{0:T(128)}, u32[]{:S(2)}) copy-start(s32[32]{0:T(128)} %param.9) | copy-start | bytes 388
  7.2 9.2 %copy-start.3 = (s32[32]{0:T(128)S(1)}, s32[32]{0:T(128)}, u32[]{:S(2)}) copy-start(s32[32]{0:T(128)} %param.10) | copy-start | bytes 388
  7.2 22.8 %copy-start.2 = (s32[32]{0:T(128)S(1)}, s32[32]{0:T(128)}, u32[]{:S(2)}) copy-start(s32[32]{0:T(128)} %param.11) | copy-start | bytes 388
  7.2 67.4 %all-gather.8.cloned.1.call-start = ((), (), s32[]{:S(2)}) async-start(), calls=%async_computation.2 | async-start | bytes 1114112 | tf_op jit(solution)/shard_map/all_gather | solution.py:17
  12.3 3.2 %copy-start.1 = (f32[4,128,32,128]{3,2,1,0:T(8,128)}, f32[4,128,32,128]{3,2,1,0:T(8,128)S(1)}, u32[]{:S(2)}) copy-start(f32[4,128,32,128]{3,2,1,0:T(8,128)S(1)} %convolution_bitcast_fusion) | copy-start | bytes 25165828
  16.3 120.9 %all-gather.6.cloned.1.call-start = ((), (), s32[]{:S(2)}) async-start(), calls=%async_computation.1 | async-start | bytes 2228224 | tf_op jit(solution)/shard_map/all_gather | solution.py:17
  16.6 35.7 %collective-permute-start = (s32[2]{0:T(128)S(1)}, s32[2]{0:T(128)S(1)}, u32[]{:S(2)}, u32[]{:S(2)}) collective-permute-start(s32[2]{0:T(128)S(1)} %get-tuple-element.291), channel_id=1, source_target_pairs={{0,2},{2,4},{4,6},{6,8},{8,10},{10,12},{12,14},{14,16},{16,18},{18... | collective-permute-start | bytes 32 | tf_op jit(solution)/shard_map/ppermute | solution.py:12
  23.2 29.2 %collective-permute-start.1 = (f32[2,128,128]{2,1,0:T(8,128)S(1)}, f32[2,128,128]{2,1,0:T(8,128)S(1)}, u32[]{:S(2)}, u32[]{:S(2)}) collective-permute-start(f32[2,128,128]{2,1,0:T(8,128)S(1)} %bitcast.81), channel_id=1, source_target_pairs={{0,2},{2,4},{4,6},{6,8},{8,10},{10,12},{12,14},{14,16},{16,18},{18... | collective-permute-start | bytes 393224 | tf_op jit(solution)/shard_map/ppermute | solution.py:12
  26.6 25.7 %collective-permute-start.2 = (s32[2]{0:T(128)S(1)}, s32[2]{0:T(128)S(1)}, u32[]{:S(2)}, u32[]{:S(2)}) collective-permute-start(s32[2]{0:T(128)S(1)} %get-tuple-element.292), channel_id=1, source_target_pairs={{2,0},{4,2},{6,4},{8,6},{10,8},{12,10},{14,12},{16,14},{18,16},{20... | collective-permute-start | bytes 32 | tf_op jit(solution)/shard_map/ppermute | solution.py:12
  27.9 24.5 %collective-permute-start.3 = (f32[2,128,128]{2,1,0:T(8,128)S(1)}, f32[2,128,128]{2,1,0:T(8,128)S(1)}, u32[]{:S(2)}, u32[]{:S(2)}) collective-permute-start(f32[2,128,128]{2,1,0:T(8,128)S(1)} %bitcast.80), channel_id=1, source_target_pairs={{2,0},{4,2},{6,4},{8,6},{10,8},{12,10},{14,12},{16,14},{18,16},{20... | collective-permute-start | bytes 393224 | tf_op jit(solution)/shard_map/ppermute | solution.py:12
  29.9 149.9 %all-reduce.6.cloned.1.call-start = ((), (), s32[]{:S(2)}) async-start(), calls=%async_computation | async-start | bytes 131072 | tf_op jit(solution)/shard_map/psum | solution.py:89
Sparse Core Ops, SparseCore 0:
  16.5 58.0 all-gather.7
  77.9 59.2 all-gather.5
  163.3 16.4 all-reduce.5
where the time goes:
time: 189 us; the launch traced here: 188 us
  waiting for transfers between devices  63.9 us (34%)
  other arithmetic  29.1 us (15%)
  local copies, waits for them, and re-layouts  27.6 us (15%)
  loops' own time  19.6 us (10%)
  blocking collectives  17.9 us (9%)
  between operations  15.2 us (8%)
  starting transfers between devices  11 us (6%)
  matrix products  3.44 us (2%)
    all_gather x2, waiting for transfers between devices, carried_in(): pieces = jax.tree.map(lambda part: lax.all_gather(part, axis), value)  52.9 us
    another operation x2, loops' own time, carried_in(): return lax.fori_loop(0, count - 1, step, running)  19.6 us
    unnamed x1, blocking collectives  17.9 us
    select_n x45, other arithmetic, step(): jnp.where(position < mine, new, old)  15.5 us
    psum x1, waiting for transfers between devices, local(): store_rollup = lax.psum(product_terms, 'prod')  10.9 us
    ppermute x4, starting transfers between devices, from_behind(): return lax.ppermute(block, axis, route)  10.9 us
    unnamed x20, local copies, waits for them, and re-layouts  9.45 us
    dynamic_slice x15, local copies, waits for them, and re-layouts, step(): longer = join(running, jax.tree.map(lambda part: part[position], pieces))  8.89 us
  transfers between devices with their start and end apart: 7, of which 3 were waited for; matrix products, arithmetic and copies ran while one was open for 13% of the time, Pallas kernels for 0%

commit v1 on v0

--- a/solution.py
+++ b/solution.py
@@ -86,7 +86,7 @@
     product_terms = jnp.concatenate(
         [jnp.sum(running, axis=0)[None], jnp.sum(levels, axis=1)], axis=0
     )
-    store_rollup = lax.psum(product_terms, "prod")
+    store_rollup = jnp.sum(lax.all_gather(product_terms, "prod"), axis=0)
     return (running, levels[0, :columns], levels[1, :columns], levels[2, :columns], store_rollup)
 
 

time: 189 us -> 174 us (0.921)
  waiting for transfers between devices: 63.9 us -> 52.9 us
  local copies, waits for them, and re-layouts: 27.6 us -> 23.2 us
  blocking collectives: 17.9 us -> 19.8 us
    psum x1 -> x0, waiting for transfers between devices: 10.9 us -> none  [local(): store_rollup = lax.psum(product_terms, 'prod')]
    squeeze x1, local copies, waits for them, and re-layouts: 5.73 us -> 2.87 us  [local(): levels[2, :columns]]
    all_gather x0 -> x1, blocking collectives: none -> 1.9 us  [local(): store_rollup = jnp.sum(lax.all_gather(product_terms, 'prod'), axis=0)]
    unnamed x20 -> x19, local copies, waits for them, and re-layouts: 9.45 us -> 7.93 us
  transfers between devices with their start and end apart: 7 -> 6, of which waited for: 3 -> 2; matrix products, arithmetic and copies ran while one was open for 13% -> 11% of each run, Pallas kernels for 0% -> 0%
where the time goes in v1:
time: 174 us; the launch traced here: 173 us
  waiting for transfers between devices  52.9 us (30%)
  other arithmetic  27.3 us (16%)
  local copies, waits for them, and re-layouts  23.2 us (13%)
  blocking collectives  19.8 us (11%)
  loops' own time  19.6 us (11%)
  between operations  15.6 us (9%)
  starting transfers between devices  10.9 us (6%)
  matrix products  3.44 us (2%)
    all_gather x2, waiting for transfers between devices, carried_in(): pieces = jax.tree.map(lambda part: lax.all_gather(part, axis), value)  52.9 us
    another operation x2, loops' own time, carried_in(): return lax.fori_loop(0, count - 1, step, running)  19.6 us
    unnamed x1, blocking collectives  17.9 us
    select_n x45, other arithmetic, step(): jnp.where(position < mine, new, old)  15.5 us
    ppermute x4, starting transfers between devices, from_behind(): return lax.ppermute(block, axis, route)  10.9 us
    dynamic_slice x15, local copies, waits for them, and re-layouts, step(): longer = join(running, jax.tree.map(lambda part: part[position], pieces))  8.86 us
    unnamed x19, local copies, waits for them, and re-layouts  7.93 us
    reduce_sum x1, other arithmetic, local(): jnp.sum(levels, axis=1)  3.58 us
  transfers between devices with their start and end apart: 6, of which 2 were waited for; matrix products, arithmetic and copies ran while one was open for 11% of the time, Pallas kernels for 0%

profile of v1, /device:TPU:0, one launch (start us, length us, event | category | flops | bytes accessed | tf_op | source)
XLA Modules:
  0.0 172.9 jit_solution(8238879962772422104)
XLA Ops:
  7.3 0.8 pad_add_fusion
  8.2 0.7 copy-done
  8.9 3.4 %convolution_bitcast_fusion = f32[4,128,32,128]{3,2,1,0:T(8,128)S(1)} fusion(f32[128,32,128]{2,1,0:T(8,128)S(1)} %copy-done, pred[3,32,32]{2,1,0:T(32,128)(4,1)S(1)} %broadcast_compare_fusion, pred[1,32,32]{2,1,0:T(32,128)(4,1)S(1)} %iota_compare_fusion), kind=kOutput, calls=%fused_computation.11 | convolution fusion | flops 805310464 | bytes 10489856 | tf_op jit(solution)/shard_map/kij,pjs->kpis/dot_general | solution.py:58
  12.3 3.2 %copy-done.1 = f32[4,128,32,128]{3,2,1,0:T(8,128)} copy-done((f32[4,128,32,128]{3,2,1,0:T(8,128)}, f32[4,128,32,128]{3,2,1,0:T(8,128)S(1)}, u32[]{:S(2)}) %copy-start.1) | copy-done | bytes 8388632
  15.5 0.8 fusion.13
  16.6 4.9 %collective-permute-start = (s32[2]{0:T(128)S(1)}, s32[2]{0:T(128)S(1)}, u32[]{:S(2)}, u32[]{:S(2)}) collective-permute-start(s32[2]{0:T(128)S(1)} %get-tuple-element.291), channel_id=1, source_target_pairs={{0,2},{2,4},{4,6},{6,8},{8,10},{10,12},{12,14},{14,16},{16,18},{18... | collective-permute-start | bytes 32 | tf_op jit(solution)/shard_map/ppermute | solution.py:12
  21.5 1.7 %fusion.12 = (f32[2,128,1,128]{3,2,1,0:T(1,128)S(1)}, f32[2,128,1,128]{3,2,1,0:T(1,128)S(1)}) fusion(f32[4,128,32,128]{3,2,1,0:T(8,128)} %copy-done.1), kind=kLoop, calls=%fused_computation.47 | loop fusion | bytes 524288 | tf_op jit(solution)/shard_map/slice | solution.py:63
  23.2 3.4 %collective-permute-start.1 = (f32[2,128,128]{2,1,0:T(8,128)S(1)}, f32[2,128,128]{2,1,0:T(8,128)S(1)}, u32[]{:S(2)}, u32[]{:S(2)}) collective-permute-start(f32[2,128,128]{2,1,0:T(8,128)S(1)} %bitcast.83), channel_id=1, source_target_pairs={{0,2},{2,4},{4,6},{6,8},{8,10},{10,12},{12,14},{14,16},{16,18},{18... | collective-permute-start | bytes 393224 | tf_op jit(solution)/shard_map/ppermute | solution.py:12
  26.6 1.3 collective-permute-start.2
  27.9 1.3 collective-permute-start.3
  29.2 0.7 pad_maximum_fusion.2
  29.9 0.6 fusion.15
  32.0 0.8 pad_dynamic-update-slice_fusion
  32.8 1.2 bitcast_dynamic-update-slice_fusion
  34.0 17.9 %all-reduce.3 = (s32[32]{0:T(128)S(1)}, s32[16]{0:T(128)S(1)}) all-reduce(s32[32]{0:T(128)S(1)} %pad_dynamic-update-slice_fusion, s32[16]{0:T(128)S(1)} %bitcast_dynamic-update-slice_fusion), channel_id=2, replica_groups=mesh['date'=16,'prod'=2] {'date'}, use_global_device_ids=true, to_apply=%add.1 | all-reduce | flops 48 | bytes 384
  52.4 0.7 broadcast_select_fusion.4
  53.1 21.4 %all-gather.9.cloned.1.call-done = f32[16,128,1,128]{3,1,2,0:T(8,128)} async-done(((f32[1,128,1,128]{3,1,2,0:T(8,128)}), f32[16,128,1,128]{3,1,2,0:T(8,128)}) %all-gather.9.cloned.1.call-update) | async-done | bytes 1048592 | tf_op jit(solution)/shard_map/all_gather | solution.py:17
  74.6 1.3 reverse_bitcast_fusion
  75.9 28.2 %while.33 = (s32[]{:T(128)}, s32[1]{0:T(128)}, f32[1,128,128]{2,1,0:T(8,128)S(1)}, s32[]{:T(128)}, s32[16,1]{0,1:T(1,128)S(1)}, /*index=5*/f32[16,1,128,128]{3,2,1,0:T(8,128)S(1)}, s32[]{:T(128)}, s32[]{:T(128)}) while((s32[]{:T(128)}, s32[1]{0:T(128)}, f32[1,128,128]{2,1,0:T(8,128)S(1)}, s32[]{:T(128)}, s32[16,1]{0,1:T(1,128)S(1)}, ...), condition=%wide.region_3.4_spmd.clone, body=%wide.region_2.3_spmd.clone.sunk | while | flops 65543 | bytes 196764 | solution.py:29
  75.9 0.6 constant_dynamic-slice_fusion.3
  77.8 0.6 constant_dynamic-slice_fusion.3
  89.1 0.6 constant_dynamic-slice_fusion.3
  90.9 0.6 constant_dynamic-slice_fusion.3
  92.8 0.6 constant_dynamic-slice_fusion.3
  104.8 0.9 pad_maximum_fusion.1
  105.7 31.4 %all-gather.7.cloned.1.call-done = f32[32,128,128]{2,1,0:T(8,128)} async-done(((f32[2,128,128]{2,1,0:T(8,128)}), f32[32,128,128]{2,1,0:T(8,128)}) %all-gather.7.cloned.1.call-update) | async-done | bytes 2097168 | tf_op jit(solution)/shard_map/all_gather | solution.py:17
  137.1 15.9 %while.32 = (s32[]{:T(128)}, s32[2]{0:T(128)S(1)}, f32[2,128,128]{2,1,0:T(8,128)S(1)}, s32[]{:T(128)}, s32[16,2]{1,0:T(8,128)S(1)}, /*index=5*/f32[16,2,128,128]{3,2,1,0:T(8,128)}, s32[]{:T(128)}, s32[]{:T(128)}) while((s32[]{:T(128)}, s32[2]{0:T(128)S(1)}, f32[2,128,128]{2,1,0:T(8,128)S(1)}, s32[]{:T(128)}, ...), condition=%wide.region_1.2_spmd.clone, body=%wide.region_0.1_spmd.clone.sunk | while | flops 131086 | bytes 393380 | solution.py:29
  137.1 1.0 fusion.18
  138.2 1.0 fusion.18
  139.3 1.0 fusion.18
  140.3 1.0 fusion.18
  141.4 1.0 fusion.18
  142.4 1.0 fusion.18
  143.5 1.0 fusion.18
  144.6 1.0 fusion.18
  145.6 1.0 fusion.18
  146.7 1.0 fusion.18
  147.8 1.0 fusion.18
  148.8 1.0 fusion.18
  149.9 1.0 fusion.18
  150.9 1.0 fusion.18
  152.0 1.0 fusion.18
  153.0 0.6 add_compare_fusion
  153.8 3.2 %fusion.8 = (f32[32,128]{1,0:T(8,128)S(1)}, f32[128,32,128]{2,1,0:T(8,128)}) fusion(f32[128,128]{1,0:T(8,128)S(1)} %get-tuple-element.332, f32[4,128,32,128]{3,2,1,0:T(8,128)} %copy-done.1), kind=kLoop, calls=%fused_computation.45 | loop fusion | flops 1044480 | bytes 4276224 | tf_op jit(solution)/shard_map/reduce_sum | solution.py:87
  157.0 3.6 %fusion.10 = (f32[3,32,128]{2,1,0:T(8,128)S(1)}, f32[3,128,32,128]{3,2,1,0:T(8,128)S(1)}) fusion(f32[3,32]{1,0:T(4,128)S(1)} %get-tuple-element.334, f32[3,128,128]{2,1,0:T(8,128)S(1)} %pad_maximum_fusion.1, f32[3,32]{1,0:T(4,128)S(1)} %get-tuple-element.333, f32[3,128,128]{2,1,0:T(8,128)S(1)} %pad_maximum_fusion, f32[4,128,32,128]{3,2,1,0:T(8,128)} %copy-done.1), kind=kLoop, calls=%fused_computation.46 | loop fusion | flops 7852032 | bytes 13026048 | tf_op jit(solution)/shard_map/reduce_sum | solution.py:87
  160.6 1.9 %all-gather.3 = f32[8,32,128]{2,1,0:T(8,128)S(1)} all-gather(f32[4,32,128]{2,1,0:T(8,128)S(1)} %pad_maximum_fusion.3), channel_id=5, replica_groups=mesh['date'=16,'prod'=2] {'prod'}, dimensions={0}, use_global_device_ids=true | all-gather | bytes 196608 | tf_op jit(solution)/shard_map/all_gather | solution.py:89
  162.5 2.9 %slice_bitcast_fusion = (f32[128,32,128]{2,1,0:T(8,128)}, f32[128,32,128]{2,1,0:T(8,128)}, f32[128,32,128]{2,1,0:T(8,128)}) fusion(f32[3,128,32,128]{3,2,1,0:T(8,128)S(1)} %get-tuple-element.322), kind=kLoop, calls=%fused_computation.12 | loop fusion | bytes 12582912 | tf_op jit(solution)/shard_map/squeeze | solution.py:90
  165.4 0.6 reduce_sum.29
  (95 shorter events, 8.4 us)
Async XLA Ops:
  7.2 1.7 copy-start
  7.2 23.6 %copy-start.5 = (u32[32]{0:T(128)S(1)}, u32[32]{0:T(128)}, u32[]{:S(2)}) copy-start(u32[32]{0:T(128)} %constant.81) | copy-start | bytes 388
  7.2 9.2 %copy-start.4 = (s32[32]{0:T(128)S(1)}, s32[32]{0:T(128)}, u32[]{:S(2)}) copy-start(s32[32]{0:T(128)} %param.9) | copy-start | bytes 388
  7.2 9.2 %copy-start.3 = (s32[32]{0:T(128)S(1)}, s32[32]{0:T(128)}, u32[]{:S(2)}) copy-start(s32[32]{0:T(128)} %param.10) | copy-start | bytes 388
  7.2 22.7 %copy-start.2 = (s32[32]{0:T(128)S(1)}, s32[32]{0:T(128)}, u32[]{:S(2)}) copy-start(s32[32]{0:T(128)} %param.11) | copy-start | bytes 388
  7.2 67.3 %all-gather.9.cloned.1.call-start = ((), (), s32[]{:S(2)}) async-start(), calls=%async_computation.1 | async-start | bytes 1114112 | tf_op jit(solution)/shard_map/all_gather | solution.py:17
  12.3 3.2 %copy-start.1 = (f32[4,128,32,128]{3,2,1,0:T(8,128)}, f32[4,128,32,128]{3,2,1,0:T(8,128)S(1)}, u32[]{:S(2)}) copy-start(f32[4,128,32,128]{3,2,1,0:T(8,128)S(1)} %convolution_bitcast_fusion) | copy-start | bytes 25165828
  16.3 120.8 %all-gather.7.cloned.1.call-start = ((), (), s32[]{:S(2)}) async-start(), calls=%async_computation | async-start | bytes 2228224 | tf_op jit(solution)/shard_map/all_gather | solution.py:17
  16.6 35.6 %collective-permute-start = (s32[2]{0:T(128)S(1)}, s32[2]{0:T(128)S(1)}, u32[]{:S(2)}, u32[]{:S(2)}) collective-permute-start(s32[2]{0:T(128)S(1)} %get-tuple-element.291), channel_id=1, source_target_pairs={{0,2},{2,4},{4,6},{6,8},{8,10},{10,12},{12,14},{14,16},{16,18},{18... | collective-permute-start | bytes 32 | tf_op jit(solution)/shard_map/ppermute | solution.py:12
  23.2 29.1 %collective-permute-start.1 = (f32[2,128,128]{2,1,0:T(8,128)S(1)}, f32[2,128,128]{2,1,0:T(8,128)S(1)}, u32[]{:S(2)}, u32[]{:S(2)}) collective-permute-start(f32[2,128,128]{2,1,0:T(8,128)S(1)} %bitcast.83), channel_id=1, source_target_pairs={{0,2},{2,4},{4,6},{6,8},{8,10},{10,12},{12,14},{14,16},{16,18},{18... | collective-permute-start | bytes 393224 | tf_op jit(solution)/shard_map/ppermute | solution.py:12
  26.6 25.6 %collective-permute-start.2 = (s32[2]{0:T(128)S(1)}, s32[2]{0:T(128)S(1)}, u32[]{:S(2)}, u32[]{:S(2)}) collective-permute-start(s32[2]{0:T(128)S(1)} %get-tuple-element.292), channel_id=1, source_target_pairs={{2,0},{4,2},{6,4},{8,6},{10,8},{12,10},{14,12},{16,14},{18,16},{20... | collective-permute-start | bytes 32 | tf_op jit(solution)/shard_map/ppermute | solution.py:12
  27.9 24.4 %collective-permute-start.3 = (f32[2,128,128]{2,1,0:T(8,128)S(1)}, f32[2,128,128]{2,1,0:T(8,128)S(1)}, u32[]{:S(2)}, u32[]{:S(2)}) collective-permute-start(f32[2,128,128]{2,1,0:T(8,128)S(1)} %bitcast.82), channel_id=1, source_target_pairs={{2,0},{4,2},{6,4},{8,6},{10,8},{12,10},{14,12},{16,14},{18,16},{20... | collective-permute-start | bytes 393224 | tf_op jit(solution)/shard_map/ppermute | solution.py:12
Sparse Core Ops, SparseCore 0:
  16.5 58.0 all-gather.8
  77.9 59.1 all-gather.6
